TPU v7x, 32 devices: a whole 2x2x4 slice. The times are simulated.
32 devices in a mesh: gx: 2 (over y), gy: 4 (over z), gz: 4 (over x, core).
Axes of the slice: x: 2, y: 2, z: 4, core: 2. Of those that a mesh axis runs over, the one named last changes fastest.
Arguments:
- forcing: float32 [3, 16, 64, 512], P(None, 'gx', 'gy', 'gz'), may hold values from -8 to 8
- viscosity: float32 [16, 64, 512], P('gx', 'gy', 'gz'), may hold values from 0.001 to 1000
Outputs:
- solution: float32 [3, 16, 64, 512], P(None, 'gx', 'gy', 'gz')
- residual: float32 [3, 16, 64, 512], P(None, 'gx', 'gy', 'gz')
All inputs are finite; a program needn't handle non-finite values.
Results may differ from a plain program's by a relative error of at most 0.00017.
Values sent between devices are 32-bit elements; how exact they have to be, the bound alone decides.
A program may use at most 64 MiB of HBM per device.

v0:
```python
import jax
import jax.numpy as jnp
from jax import lax
from jax.sharding import PartitionSpec as P

ITERS = 3
CSWEEPS = 4
reaction = 1.0
relaxation = 2.0 / 3.0
neighbours = ((1, 0, 0), (-1, 0, 0), (0, 1, 0), (0, -1, 0), (0, 0, 1), (0, 0, -1))


def with_halo(x, sides, width):
    for axis, dim in sides:
        count, length = (lax.axis_size(axis), x.shape[dim])
        up = [(i, (i + 1) % count) for i in range(count - 1)]
        down = [(j, i) for i, j in up]
        last = lax.slice_in_dim(x, length - width, length, axis=dim)
        initial = lax.slice_in_dim(x, 0, width, axis=dim)
        before = lax.ppermute(last, axis, up)
        after = lax.ppermute(initial, axis, down)
        x = jnp.concatenate([before, x, after], axis=dim)
    return x


def window(padded, offset, extent):
    return padded[
        ...,
        1 + offset[0] : 1 + offset[0] + extent[0],
        1 + offset[1] : 1 + offset[1] + extent[1],
        1 + offset[2] : 1 + offset[2] + extent[2],
    ]


def viscous(values, padded_values, viscosity, padded_visc, mass_term, face_term):
    extent = viscosity.shape
    summed = mass_term * values
    for offset in neighbours:
        beside = window(padded_visc, offset, extent)
        across = window(padded_values, offset, extent)
        summed = summed + face_term * (viscosity + beside) * (values - across)
    return summed


def diagonal_of(viscosity, padded_visc, mass_term, face_term):
    summed = jnp.full(viscosity.shape, mass_term, jnp.float32)
    for offset in neighbours:
        summed = summed + face_term * (viscosity + window(padded_visc, offset, viscosity.shape))
    return summed


def restrict(values):
    extent = values.shape
    return values.reshape(extent[0], extent[1] // 2, 2, extent[2] // 2, 2, extent[3] // 2, 2).sum(
        axis=(2, 4, 6)
    )


def prolong(values):
    return jnp.repeat(jnp.repeat(jnp.repeat(values, 2, axis=1), 2, axis=2), 2, axis=3)


def coarsen(viscosity):
    extent = viscosity.shape
    return viscosity.reshape(extent[0] // 2, 2, extent[1] // 2, 2, extent[2] // 2, 2).mean(
        axis=(1, 3, 5)
    )


def sweeps(coarse_rhs, diagonal, applier):
    correction = relaxation * coarse_rhs / diagonal
    for counter in range(CSWEEPS - 1):
        correction = correction + relaxation * (coarse_rhs - applier(correction)) / diagonal
    return correction


def precond_product(residual, precond):
    return lax.psum(jnp.sum(residual * precond), ("gx", "gy", "gz"))


def shards(forcing, viscosity):
    padded_visc = with_halo(viscosity, (("gx", 0), ("gy", 1), ("gz", 2)), 1)
    fine_diag = diagonal_of(viscosity, padded_visc, reaction, 0.5)
    coarse_visc = coarsen(viscosity)

    def fine_apply(values):
        padded = with_halo(values, (("gx", 1), ("gy", 2), ("gz", 3)), 1)
        return viscous(values, padded, viscosity, padded_visc, reaction, 0.5)

    group_visc = lax.all_gather(coarse_visc, "gz", axis=2, tiled=True)
    group_pad = with_halo(group_visc, (("gx", 0), ("gy", 1)), 1)
    group_pad = jnp.pad(group_pad, ((0, 0), (0, 0), (1, 1)))
    group_diag = diagonal_of(group_visc, group_pad, 8.0 * reaction, 2.0)
    depth_local = coarse_visc.shape[2]
    offset_z = lax.axis_index("gz") * depth_local

    def group_apply(values):
        padded = with_halo(values, (("gx", 1), ("gy", 2)), 1)
        padded = jnp.pad(padded, ((0, 0), (0, 0), (0, 0), (1, 1)))
        return viscous(values, padded, group_visc, group_pad, 8.0 * reaction, 2.0)

    def coarse_solve(coarse_rhs):
        whole_line = lax.all_gather(coarse_rhs, "gz", axis=3, tiled=True)
        correction = sweeps(whole_line, group_diag, group_apply)
        return lax.dynamic_slice_in_dim(correction, offset_z, depth_local, 3)

    def precondition(residual):
        smoothed = relaxation * residual / fine_diag
        defect = residual - fine_apply(smoothed)
        correction = coarse_solve(restrict(defect))
        smoothed = smoothed + prolong(correction)
        return smoothed + relaxation * (residual - fine_apply(smoothed)) / fine_diag

    solution = jnp.zeros_like(forcing)
    residual = forcing
    precond = precondition(residual)
    product = precond_product(residual, precond)
    direction = precond
    for iteration in range(ITERS):
        applied = fine_apply(direction)
        alpha_step = product / lax.psum(jnp.sum(direction * applied), ("gx", "gy", "gz"))
        solution = solution + alpha_step * direction
        residual = residual - alpha_step * applied
        if iteration + 1 < ITERS:
            precond = precondition(residual)
            product_next = precond_product(residual, precond)
            direction = precond + product_next / product * direction
            product = product_next
    return (solution, residual)


def solution(mesh):
    return jax.shard_map(
        shards,
        mesh=mesh,
        in_specs=(P(None, "gx", "gy", "gz"), P("gx", "gy", "gz")),
        out_specs=(P(None, "gx", "gy", "gz"), P(None, "gx", "gy", "gz")),
        check_vma=False,
    )
```

profile of v0, /device:TPU:0, one launch (start us, length us, event | category | flops | bytes accessed | tf_op | source)
XLA Modules:
  0.0 754.0 jit_solution(5678509347087031177)
XLA Ops:
  1.3 4.9 collective-permute-start.1
  7.5 6.3 reshape.58
  21.4 7.2 all_gather.13
  32.5 4.5 collective-permute-start.13
  38.6 4.5 collective-permute-start.7
  44.5 4.5 collective-permute-start.15
  50.4 4.5 collective-permute-start.9
  66.7 13.9 %reshape.57 = f32[3,4,2,8,2,64,2]{6,5,4,3,2,1,0:T(8,128)} reshape(f32[3,8,16,128]{3,2,1,0:T(8,128)S(1)} %fusion.162) | data formatting | bytes 393216 | tf_op jit(solution)/shard_map/reshape | solution.py:54
  80.7 5.5 reduce_sum.90
  86.4 19.3 %all_gather.12 = f32[3,4,8,256]{2,1,0,3:T(4,128)S(1)} all-gather(f32[3,4,8,64]{2,1,0,3:T(4,128)S(1)} %copy.996), channel_id=1, replica_groups=mesh['gx'=2,'gy'=4,'gz'=4] {'gz'}, dimensions={3}, use_global_device_ids=true | all-gather | bytes 122880 | tf_op jit(solution)/shard_map/all_gather | solution.py:103
  106.3 4.5 collective-permute-start.17
  204.8 46.7 %all-reduce.10 = (f32[]{:T(128)}, f32[]{:T(128)}) all-reduce(f32[]{:T(128)} %get-tuple-element.13, f32[]{:T(128)} %get-tuple-element.12), channel_id=1, replica_groups=mesh['gx'=2,'gy'=4,'gz'=4] {'gx','gy','gz'}, use_global_device_ids=true, to_apply=%region_3.4 | all-reduce | flops 2 | bytes 16 | tf_op jit(solution)/shard_map/psum | solution.py:78
  278.6 13.9 %reshape.62 = f32[3,4,2,8,2,64,2]{6,5,4,3,2,1,0:T(8,128)} reshape(f32[3,8,16,128]{3,2,1,0:T(8,128)S(1)} %fusion.103) | data formatting | bytes 393216 | tf_op jit(solution)/shard_map/reshape | solution.py:54
  292.6 5.5 reduce_sum.94
  298.3 18.5 %all_gather.14 = f32[3,4,8,256]{2,1,0,3:T(4,128)S(1)} all-gather(f32[3,4,8,64]{2,1,0,3:T(4,128)S(1)} %copy.1016), channel_id=1, replica_groups=mesh['gx'=2,'gy'=4,'gz'=4] {'gz'}, dimensions={3}, use_global_device_ids=true | all-gather | bytes 122880 | tf_op jit(solution)/shard_map/all_gather | solution.py:103
  389.3 41.5 %psum.44 = f32[]{:T(128)} all-reduce(f32[]{:T(128)} %get-tuple-element.24), channel_id=1, replica_groups=mesh['gx'=2,'gy'=4,'gz'=4] {'gx','gy','gz'}, use_global_device_ids=true, to_apply=%region_8.9 | all-reduce | flops 1 | bytes 8 | tf_op jit(solution)/shard_map/psum | solution.py:78
  432.1 4.4 collective-permute-start.65
  458.5 43.7 %psum.45 = f32[]{:T(128)} all-reduce(f32[]{:T(128)} %get-tuple-element.22), channel_id=1, replica_groups=mesh['gx'=2,'gy'=4,'gz'=4] {'gx','gy','gz'}, use_global_device_ids=true, to_apply=%region_10.11 | all-reduce | flops 1 | bytes 8 | tf_op jit(solution)/shard_map/psum | solution.py:121
  503.6 4.4 collective-permute-start.71
  528.8 13.9 %reshape.66 = f32[3,4,2,8,2,64,2]{6,5,4,3,2,1,0:T(8,128)} reshape(f32[3,8,16,128]{3,2,1,0:T(8,128)S(1)} %fusion.44) | data formatting | bytes 393216 | tf_op jit(solution)/shard_map/reshape | solution.py:54
  542.8 5.5 reduce_sum.97
  548.5 18.5 %all_gather.15 = f32[3,4,8,256]{2,1,0,3:T(4,128)S(1)} all-gather(f32[3,4,8,64]{2,1,0,3:T(4,128)S(1)} %copy.1024), channel_id=1, replica_groups=mesh['gx'=2,'gy'=4,'gz'=4] {'gz'}, dimensions={3}, use_global_device_ids=true | all-gather | bytes 122880 | tf_op jit(solution)/shard_map/all_gather | solution.py:103
  638.3 41.5 %psum.46 = f32[]{:T(128)} all-reduce(f32[]{:T(128)} %get-tuple-element.18), channel_id=1, replica_groups=mesh['gx'=2,'gy'=4,'gz'=4] {'gx','gy','gz'}, use_global_device_ids=true, to_apply=%region_13.14 | all-reduce | flops 1 | bytes 8 | tf_op jit(solution)/shard_map/psum | solution.py:78
  707.5 43.7 %psum.47 = f32[]{:T(128)} all-reduce(f32[]{:T(128)} %get-tuple-element.16), channel_id=1, replica_groups=mesh['gx'=2,'gy'=4,'gz'=4] {'gx','gy','gz'}, use_global_device_ids=true, to_apply=%region_15.16 | all-reduce | flops 1 | bytes 8 | tf_op jit(solution)/shard_map/psum | solution.py:121
  (341 shorter events, 363.4 us)
Async XLA Ops:
  1.3 15.2 %collective-permute-start.1 = (f32[1,16,128]{2,1,0:T(8,128)S(1)}, f32[1,16,128]{2,1,0:T(8,128)S(1)}, u32[]{:S(2)}, u32[]{:S(2)}) collective-permute-start(f32[1,16,128]{2,1,0:T(8,128)S(1)} %get-tuple-element.143), channel_id=1, source_target_pairs={{0,16},{1,17},{2,18},{3,19},{4,20},{5,21},{6,22},{7,23},{8,24},{9,... | collective-permute-start | bytes 24584 | tf_op jit(solution)/shard_map/ppermute | solution.py:20
  6.2 10.4 %collective-permute-start = (f32[1,16,128]{2,1,0:T(8,128)S(1)}, f32[1,16,128]{2,1,0:T(8,128)S(1)}, u32[]{:S(2)}, u32[]{:S(2)}) collective-permute-start(f32[1,16,128]{2,1,0:T(8,128)S(1)} %get-tuple-element.144), channel_id=1, source_target_pairs={{16,0},{17,1},{18,2},{19,3},{20,4},{21,5},{22,6},{23,7},{24,8},{25... | collective-permute-start | bytes 24584 | tf_op jit(solution)/shard_map/ppermute | solution.py:21
  16.6 12.1 %collective-permute-start.3 = (f32[10,1,128]{2,1,0:T(1,128)S(1)}, f32[10,1,128]{2,1,0:T(1,128)S(1)}, u32[]{:S(2)}, u32[]{:S(2)}) collective-permute-start(f32[10,1,128]{2,1,0:T(1,128)S(1)} %get-tuple-element.141), channel_id=1, source_target_pairs={{0,4},{4,8},{8,12},{1,5},{5,9},{9,13},{2,6},{6,10},{10,14},{3,7},{... | collective-permute-start | bytes 15368 | tf_op jit(solution)/shard_map/ppermute | solution.py:20
  20.1 8.7 %collective-permute-start.2 = (f32[10,1,128]{2,1,0:T(1,128)S(1)}, f32[10,1,128]{2,1,0:T(1,128)S(1)}, u32[]{:S(2)}, u32[]{:S(2)}) collective-permute-start(f32[10,1,128]{2,1,0:T(1,128)S(1)} %get-tuple-element.142), channel_id=1, source_target_pairs={{4,0},{8,4},{12,8},{5,1},{9,5},{13,9},{6,2},{10,6},{14,10},{7,3},{... | collective-permute-start | bytes 15368 | tf_op jit(solution)/shard_map/ppermute | solution.py:21
  28.9 9.4 %collective-permute-start.5 = (f32[10,18,1]{2,1,0:T(8,128)S(1)}, f32[10,18,1]{2,1,0:T(8,128)S(1)}, u32[]{:S(2)}, u32[]{:S(2)}) collective-permute-start(f32[10,18,1]{2,1,0:T(8,128)S(1)} %get-tuple-element.121), channel_id=1, source_target_pairs={{0,1},{1,2},{2,3},{4,5},{5,6},{6,7},{8,9},{9,10},{10,11},{12,13},{... | collective-permute-start | bytes 2168 | tf_op jit(solution)/shard_map/ppermute | solution.py:20
  31.2 7.2 collective-permute-start.4
  32.5 11.9 %collective-permute-start.13 = (f32[1,8,256]{2,1,0:T(8,128)S(1)}, f32[1,8,256]{2,1,0:T(8,128)S(1)}, u32[]{:S(2)}, u32[]{:S(2)}) collective-permute-start(f32[1,8,256]{2,1,0:T(8,128)S(1)} %get-tuple-element.147), channel_id=1, source_target_pairs={{0,16},{1,17},{2,18},{3,19},{4,20},{5,21},{6,22},{7,23},{8,24},{9,... | collective-permute-start | bytes 24584 | tf_op jit(solution)/shard_map/ppermute | solution.py:20
  37.0 7.4 collective-permute-start.12
  38.6 11.7 %collective-permute-start.7 = (f32[3,1,16,128]{3,2,1,0:T(8,128)S(1)}, f32[3,1,16,128]{3,2,1,0:T(8,128)S(1)}, u32[]{:S(2)}, u32[]{:S(2)}) collective-permute-start(f32[3,1,16,128]{3,2,1,0:T(8,128)S(1)} %get-tuple-element.101), channel_id=1, source_target_pairs={{0,16},{1,17},{2,18},{3,19},{4,20},{5,21},{6,22},{7,23},{8,24},{9,... | collective-permute-start | bytes 73736 | tf_op jit(solution)/shard_map/ppermute | solution.py:20
  43.1 7.2 collective-permute-start.6
  44.5 11.8 %collective-permute-start.15 = (f32[6,1,256]{2,1,0:T(1,128)S(1)}, f32[6,1,256]{2,1,0:T(1,128)S(1)}, u32[]{:S(2)}, u32[]{:S(2)}) collective-permute-start(f32[6,1,256]{2,1,0:T(1,128)S(1)} %get-tuple-element.145), channel_id=1, source_target_pairs={{0,4},{4,8},{8,12},{1,5},{5,9},{9,13},{2,6},{6,10},{10,14},{3,7},{... | collective-permute-start | bytes 18440 | tf_op jit(solution)/shard_map/ppermute | solution.py:20
  49.0 7.2 collective-permute-start.14
  50.4 6.0 collective-permute-start.9
  106.3 6.1 collective-permute-start.17
  110.9 5.7 collective-permute-start.16
  127.9 5.7 collective-permute-start.20
  184.7 5.7 collective-permute-start.34
  252.9 5.9 collective-permute-start.41
  369.2 5.7 collective-permute-start.58
  432.1 5.9 collective-permute-start.65
  436.6 5.7 collective-permute-start.64
  503.6 5.9 collective-permute-start.71
  569.2 5.7 collective-permute-start.76
  681.1 5.9 collective-permute-start.95
  (80 other events, 421.1 us)
where the time goes:
time: 757 us; the launch traced here: 754 us
  blocking collectives  281 us (37%)
  starting transfers between devices  208 us (27%)
  waiting for transfers between devices  164 us (22%)
  local copies, waits for them, and re-layouts  60.2 us (8%)
  other arithmetic  32.7 us (4%)
  between operations  8.96 us (1%)
    ppermute x50, waiting for transfers between devices, with_halo(): after = lax.ppermute(initial, axis, down)  147 us
    ppermute x50, starting transfers between devices, with_halo(): before = lax.ppermute(last, axis, up)  143 us
    psum x3, blocking collectives, precond_product(): return lax.psum(jnp.sum(residual * precond), ('gx', 'gy', 'gz'))  130 us
    psum x2, blocking collectives, shards(): lax.psum(jnp.sum(direction * applied), ('gx', 'gy', 'gz'))  87.4 us
    ppermute x50, starting transfers between devices, with_halo(): after = lax.ppermute(initial, axis, down)  64.8 us
    all_gather x3, blocking collectives, coarse_solve(): whole_line = lax.all_gather(coarse_rhs, 'gz', axis=3, tiled=True)  56.3 us
    reshape x3, local copies, waits for them, and re-layouts, restrict(): values.reshape(extent[0], extent[1] // 2, 2, extent[2] // 2, 2, extent[3]...  41.8 us
    ppermute x50, waiting for transfers between devices, with_halo(): before = lax.ppermute(last, axis, up)  16.6 us
  transfers between devices with their start and end apart: 100, of which 77 were waited for; matrix products, arithmetic and copies ran while one was open for 1% of the time, Pallas kernels for 0%

commit v1 on v0

--- a/solution.py
+++ b/solution.py
@@ -100,7 +100,7 @@
         return viscous(values, padded, group_visc, group_pad, 8.0 * reaction, 2.0)
 
     def coarse_solve(coarse_rhs):
-        whole_line = lax.all_gather(coarse_rhs, "gz", axis=3, tiled=True)
+        whole_line = jnp.concatenate(lax.all_gather(coarse_rhs, "gz"), axis=3)
         correction = sweeps(whole_line, group_diag, group_apply)
         return lax.dynamic_slice_in_dim(correction, offset_z, depth_local, 3)
 

time: 757 us -> 738 us (0.975)
  blocking collectives: 281 us -> 261 us
    all_gather x3, blocking collectives: 56.3 us -> 33.9 us  [coarse_solve(): whole_line = jnp.concatenate(lax.all_gather(coarse_rhs, 'gz'), axis=3)]
where the time goes in v1:
time: 738 us; the launch traced here: 735 us
  blocking collectives  261 us (35%)
  starting transfers between devices  209 us (28%)
  waiting for transfers between devices  164 us (22%)
  local copies, waits for them, and re-layouts  58.7 us (8%)
  other arithmetic  33.6 us (5%)
  between operations  8.84 us (1%)
    ppermute x50, waiting for transfers between devices, with_halo(): after = lax.ppermute(initial, axis, down)  147 us
    ppermute x50, starting transfers between devices, with_halo(): before = lax.ppermute(last, axis, up)  144 us
    psum x3, blocking collectives, precond_product(): return lax.psum(jnp.sum(residual * precond), ('gx', 'gy', 'gz'))  132 us
    psum x2, blocking collectives, shards(): lax.psum(jnp.sum(direction * applied), ('gx', 'gy', 'gz'))  87.4 us
    ppermute x50, starting transfers between devices, with_halo(): after = lax.ppermute(initial, axis, down)  64.9 us
    reshape x3, local copies, waits for them, and re-layouts, restrict(): values.reshape(extent[0], extent[1] // 2, 2, extent[2] // 2, 2, extent[3]...  41.8 us
    all_gather x3, blocking collectives, coarse_solve(): whole_line = jnp.concatenate(lax.all_gather(coarse_rhs, 'gz'), axis=3)  33.9 us
    ppermute x50, waiting for transfers between devices, with_halo(): before = lax.ppermute(last, axis, up)  16.6 us
  transfers between devices with their start and end apart: 100, of which 77 were waited for; matrix products, arithmetic and copies ran while one was open for 1% of the time, Pallas kernels for 0%

profile of v1, /device:TPU:0, one launch (start us, length us, event | category | flops | bytes accessed | tf_op | source)
XLA Modules:
  0.0 734.8 jit_solution(9551145757115760928)
XLA Ops:
  1.3 4.9 collective-permute-start.1
  7.7 6.3 reshape.78
  21.6 7.2 all_gather.23
  32.6 4.5 collective-permute-start.13
  38.7 4.5 collective-permute-start.7
  44.6 4.5 collective-permute-start.15
  50.5 4.5 collective-permute-start.9
  66.9 13.9 %reshape.75 = f32[3,4,2,8,2,64,2]{6,5,4,3,2,1,0:T(8,128)} reshape(f32[3,8,16,128]{3,2,1,0:T(8,128)S(1)} %fusion.162) | data formatting | bytes 393216 | tf_op jit(solution)/shard_map/reshape | solution.py:54
  80.8 5.5 reduce_sum.90
  86.3 11.9 %all-gather = f32[12,4,8,64]{3,2,1,0:T(8,128)S(1)} all-gather(f32[3,4,8,64]{3,2,1,0:T(8,128)S(1)} %reduce_sum.90), channel_id=2, replica_groups=mesh['gx'=2,'gy'=4,'gz'=4] {'gz'}, dimensions={0}, use_global_device_ids=true | all-gather | bytes 122880 | tf_op jit(solution)/shard_map/all_gather | solution.py:103
  98.5 4.5 collective-permute-start.17
  198.0 46.9 %all-reduce.10 = (f32[]{:T(128)}, f32[]{:T(128)}) all-reduce(f32[]{:T(128)} %get-tuple-element.13, f32[]{:T(128)} %get-tuple-element.12), channel_id=1, replica_groups=mesh['gx'=2,'gy'=4,'gz'=4] {'gx','gy','gz'}, use_global_device_ids=true, to_apply=%region_3.4 | all-reduce | flops 2 | bytes 16 | tf_op jit(solution)/shard_map/psum | solution.py:78
  272.1 13.9 %reshape.82 = f32[3,4,2,8,2,64,2]{6,5,4,3,2,1,0:T(8,128)} reshape(f32[3,8,16,128]{3,2,1,0:T(8,128)S(1)} %fusion.103) | data formatting | bytes 393216 | tf_op jit(solution)/shard_map/reshape | solution.py:54
  286.0 5.5 reduce_sum.94
  291.5 11.0 %all-gather.1 = f32[12,4,8,64]{3,2,1,0:T(8,128)S(1)} all-gather(f32[3,4,8,64]{3,2,1,0:T(8,128)S(1)} %reduce_sum.94), channel_id=3, replica_groups=mesh['gx'=2,'gy'=4,'gz'=4] {'gz'}, dimensions={0}, use_global_device_ids=true | all-gather | bytes 122880 | tf_op jit(solution)/shard_map/all_gather | solution.py:103
  374.8 42.8 %psum.44 = f32[]{:T(128)} all-reduce(f32[]{:T(128)} %get-tuple-element.24), channel_id=1, replica_groups=mesh['gx'=2,'gy'=4,'gz'=4] {'gx','gy','gz'}, use_global_device_ids=true, to_apply=%region_8.9 | all-reduce | flops 1 | bytes 8 | tf_op jit(solution)/shard_map/psum | solution.py:78
  418.9 4.4 collective-permute-start.65
  445.3 43.7 %psum.45 = f32[]{:T(128)} all-reduce(f32[]{:T(128)} %get-tuple-element.22), channel_id=1, replica_groups=mesh['gx'=2,'gy'=4,'gz'=4] {'gx','gy','gz'}, use_global_device_ids=true, to_apply=%region_10.11 | all-reduce | flops 1 | bytes 8 | tf_op jit(solution)/shard_map/psum | solution.py:121
  490.4 4.4 collective-permute-start.71
  515.6 13.9 %reshape.88 = f32[3,4,2,8,2,64,2]{6,5,4,3,2,1,0:T(8,128)} reshape(f32[3,8,16,128]{3,2,1,0:T(8,128)S(1)} %fusion.44) | data formatting | bytes 393216 | tf_op jit(solution)/shard_map/reshape | solution.py:54
  529.5 5.5 reduce_sum.97
  535.0 11.0 %all-gather.2 = f32[12,4,8,64]{3,2,1,0:T(8,128)S(1)} all-gather(f32[3,4,8,64]{3,2,1,0:T(8,128)S(1)} %reduce_sum.97), channel_id=4, replica_groups=mesh['gx'=2,'gy'=4,'gz'=4] {'gz'}, dimensions={0}, use_global_device_ids=true | all-gather | bytes 122880 | tf_op jit(solution)/shard_map/all_gather | solution.py:103
  617.9 42.8 %psum.46 = f32[]{:T(128)} all-reduce(f32[]{:T(128)} %get-tuple-element.18), channel_id=1, replica_groups=mesh['gx'=2,'gy'=4,'gz'=4] {'gx','gy','gz'}, use_global_device_ids=true, to_apply=%region_13.14 | all-reduce | flops 1 | bytes 8 | tf_op jit(solution)/shard_map/psum | solution.py:78
  688.5 43.7 %psum.47 = f32[]{:T(128)} all-reduce(f32[]{:T(128)} %get-tuple-element.16), channel_id=1, replica_groups=mesh['gx'=2,'gy'=4,'gz'=4] {'gx','gy','gz'}, use_global_device_ids=true, to_apply=%region_15.16 | all-reduce | flops 1 | bytes 8 | tf_op jit(solution)/shard_map/psum | solution.py:121
  (341 shorter events, 364.0 us)
Async XLA Ops:
  1.3 15.3 %collective-permute-start.1 = (f32[1,16,128]{2,1,0:T(8,128)S(1)}, f32[1,16,128]{2,1,0:T(8,128)S(1)}, u32[]{:S(2)}, u32[]{:S(2)}) collective-permute-start(f32[1,16,128]{2,1,0:T(8,128)S(1)} %get-tuple-element.143), channel_id=1, source_target_pairs={{0,16},{1,17},{2,18},{3,19},{4,20},{5,21},{6,22},{7,23},{8,24},{9,... | collective-permute-start | bytes 24584 | tf_op jit(solution)/shard_map/ppermute | solution.py:20
  6.3 10.5 %collective-permute-start = (f32[1,16,128]{2,1,0:T(8,128)S(1)}, f32[1,16,128]{2,1,0:T(8,128)S(1)}, u32[]{:S(2)}, u32[]{:S(2)}) collective-permute-start(f32[1,16,128]{2,1,0:T(8,128)S(1)} %get-tuple-element.144), channel_id=1, source_target_pairs={{16,0},{17,1},{18,2},{19,3},{20,4},{21,5},{22,6},{23,7},{24,8},{25... | collective-permute-start | bytes 24584 | tf_op jit(solution)/shard_map/ppermute | solution.py:21
  16.8 12.1 %collective-permute-start.3 = (f32[10,1,128]{2,1,0:T(1,128)S(1)}, f32[10,1,128]{2,1,0:T(1,128)S(1)}, u32[]{:S(2)}, u32[]{:S(2)}) collective-permute-start(f32[10,1,128]{2,1,0:T(1,128)S(1)} %get-tuple-element.141), channel_id=1, source_target_pairs={{0,4},{4,8},{8,12},{1,5},{5,9},{9,13},{2,6},{6,10},{10,14},{3,7},{... | collective-permute-start | bytes 15368 | tf_op jit(solution)/shard_map/ppermute | solution.py:20
  20.3 8.7 %collective-permute-start.2 = (f32[10,1,128]{2,1,0:T(1,128)S(1)}, f32[10,1,128]{2,1,0:T(1,128)S(1)}, u32[]{:S(2)}, u32[]{:S(2)}) collective-permute-start(f32[10,1,128]{2,1,0:T(1,128)S(1)} %get-tuple-element.142), channel_id=1, source_target_pairs={{4,0},{8,4},{12,8},{5,1},{9,5},{13,9},{6,2},{10,6},{14,10},{7,3},{... | collective-permute-start | bytes 15368 | tf_op jit(solution)/shard_map/ppermute | solution.py:21
  29.1 9.4 %collective-permute-start.5 = (f32[10,18,1]{2,1,0:T(8,128)S(1)}, f32[10,18,1]{2,1,0:T(8,128)S(1)}, u32[]{:S(2)}, u32[]{:S(2)}) collective-permute-start(f32[10,18,1]{2,1,0:T(8,128)S(1)} %get-tuple-element.121), channel_id=1, source_target_pairs={{0,1},{1,2},{2,3},{4,5},{5,6},{6,7},{8,9},{9,10},{10,11},{12,13},{... | collective-permute-start | bytes 2168 | tf_op jit(solution)/shard_map/ppermute | solution.py:20
  31.3 7.2 collective-permute-start.4
  32.6 11.9 %collective-permute-start.13 = (f32[1,8,256]{2,1,0:T(8,128)S(1)}, f32[1,8,256]{2,1,0:T(8,128)S(1)}, u32[]{:S(2)}, u32[]{:S(2)}) collective-permute-start(f32[1,8,256]{2,1,0:T(8,128)S(1)} %get-tuple-element.147), channel_id=1, source_target_pairs={{0,16},{1,17},{2,18},{3,19},{4,20},{5,21},{6,22},{7,23},{8,24},{9,... | collective-permute-start | bytes 24584 | tf_op jit(solution)/shard_map/ppermute | solution.py:20
  37.2 7.4 %collective-permute-start.12 = (f32[1,8,256]{2,1,0:T(8,128)S(1)}, f32[1,8,256]{2,1,0:T(8,128)S(1)}, u32[]{:S(2)}, u32[]{:S(2)}) collective-permute-start(f32[1,8,256]{2,1,0:T(8,128)S(1)} %get-tuple-element.148), channel_id=1, source_target_pairs={{16,0},{17,1},{18,2},{19,3},{20,4},{21,5},{22,6},{23,7},{24,8},{25... | collective-permute-start | bytes 24584 | tf_op jit(solution)/shard_map/ppermute | solution.py:21
  38.7 11.7 %collective-permute-start.7 = (f32[3,1,16,128]{3,2,1,0:T(8,128)S(1)}, f32[3,1,16,128]{3,2,1,0:T(8,128)S(1)}, u32[]{:S(2)}, u32[]{:S(2)}) collective-permute-start(f32[3,1,16,128]{3,2,1,0:T(8,128)S(1)} %get-tuple-element.101), channel_id=1, source_target_pairs={{0,16},{1,17},{2,18},{3,19},{4,20},{5,21},{6,22},{7,23},{8,24},{9,... | collective-permute-start | bytes 73736 | tf_op jit(solution)/shard_map/ppermute | solution.py:20
  43.3 7.2 collective-permute-start.6
  44.6 11.8 %collective-permute-start.15 = (f32[6,1,256]{2,1,0:T(1,128)S(1)}, f32[6,1,256]{2,1,0:T(1,128)S(1)}, u32[]{:S(2)}, u32[]{:S(2)}) collective-permute-start(f32[6,1,256]{2,1,0:T(1,128)S(1)} %get-tuple-element.145), channel_id=1, source_target_pairs={{0,4},{4,8},{8,12},{1,5},{5,9},{9,13},{2,6},{6,10},{10,14},{3,7},{... | collective-permute-start | bytes 18440 | tf_op jit(solution)/shard_map/ppermute | solution.py:20
  49.2 7.2 collective-permute-start.14
  50.5 6.0 collective-permute-start.9
  98.5 6.1 collective-permute-start.17
  103.1 5.7 collective-permute-start.16
  120.1 5.7 collective-permute-start.20
  137.0 5.7 collective-permute-start.24
  246.3 5.9 collective-permute-start.41
  320.6 5.7 collective-permute-start.50
  418.9 5.9 collective-permute-start.65
  423.3 5.7 collective-permute-start.64
  490.4 5.9 collective-permute-start.71
  548.0 5.7 collective-permute-start.76
  662.0 5.9 collective-permute-start.95
  (80 other events, 550.4 us)
